TPU v7x, 32 devices: a whole 2x2x4 slice. The times are simulated.
32 devices in a mesh: dp: 8 (over z, core), tensor: 4 (over y, x).
Axes of the slice: x: 2, y: 2, z: 4, core: 2. Of those that a mesh axis runs over, the one named last changes fastest.
Arguments:
- tokens: bfloat16 [1024, 2048], P(('dp', 'tensor')), may hold values from -6 to 6
- gate_weight: bfloat16 [2048, 8192], P(None, 'tensor'), may hold values from -0.125 to 0.125
- up_act: bfloat16 [1024, 8192], P('dp', 'tensor'), may hold values from -6 to 6
- cotangent: bfloat16 [1024, 8192], P('dp', 'tensor'), may hold values from -6 to 6
- moment1: bfloat16 [2048, 8192], P('dp', 'tensor'), may hold values from -0.359375 to 0.359375
- moment2: bfloat16 [2048, 8192], P('dp', 'tensor'), may hold values from 0.0039978027 to 0.039794922
Outputs:
- in_grad: bfloat16 [1024, 2048], P(('dp', 'tensor'))
- up_grad: bfloat16 [1024, 8192], P('dp', 'tensor')
- new_moment1: bfloat16 [2048, 8192], P('dp', 'tensor')
- new_moment2: bfloat16 [2048, 8192], P('dp', 'tensor')
- update: float32 [2048, 8192], P('dp', 'tensor')
All inputs are finite; a program needn't handle non-finite values.
Results may differ from a plain program's by a relative error of at most 0.015.
Values may be sent and summed in bfloat16 or wider, within the bound.
A program may use at most 64 MiB of HBM per device.

v0:
```python
import math

import jax
import jax.numpy as jnp
from jax import lax
from jax.sharding import PartitionSpec as P


def local(tokens, gate_weight, up_act, cotangent, moment1, moment2):
    gathered = lax.all_gather(tokens, "tensor", axis=0, tiled=True)
    gate_pre = jnp.dot(gathered, gate_weight, preferred_element_type=jnp.float32)
    sigmoid_gate = jax.nn.sigmoid(gate_pre)
    cot_float = cotangent.astype(jnp.float32)
    up_grad = (cot_float * gate_pre * sigmoid_gate).astype(jnp.bfloat16)
    gate_grad = (
        cot_float
        * up_act.astype(jnp.float32)
        * sigmoid_gate
        * (1.0 + gate_pre * (1.0 - sigmoid_gate))
    ).astype(jnp.bfloat16)
    in_grad = lax.psum_scatter(
        lax.dot_general(
            gate_grad, gate_weight, (((1,), (1,)), ((), ())), preferred_element_type=jnp.float32
        ).astype(jnp.bfloat16),
        "tensor",
        scatter_dimension=0,
        tiled=True,
    )
    partial_value = lax.dot_general(
        gathered, gate_grad, (((0,), (0,)), ((), ())), preferred_element_type=jnp.float32
    ).astype(jnp.bfloat16)
    grad_shard = lax.psum_scatter(
        partial_value.astype(jnp.float32), "dp", scatter_dimension=0, tiled=True
    )
    grad_scale = 1.0 / math.sqrt(lax.axis_size("dp") * gathered.shape[0])
    grad = grad_shard * grad_scale
    first = 0.9 * moment1.astype(jnp.float32) + 0.1 * grad
    second = 0.95 * moment2.astype(jnp.float32) + 0.05 * grad * grad
    update = first / (jnp.sqrt(second) + 1e-08)
    return (in_grad, up_grad, first.astype(jnp.bfloat16), second.astype(jnp.bfloat16), update)


def solution(mesh):
    placed = (
        P(("dp", "tensor"), None),
        P(None, "tensor"),
        P("dp", "tensor"),
        P("dp", "tensor"),
        P("dp", "tensor"),
        P("dp", "tensor"),
    )
    return jax.shard_map(
        local,
        mesh=mesh,
        in_specs=placed,
        out_specs=(
            P(("dp", "tensor"), None),
            P("dp", "tensor"),
            P("dp", "tensor"),
            P("dp", "tensor"),
            P("dp", "tensor"),
        ),
        check_vma=False,
    )
```

profile of v0, /device:TPU:0, one launch (start us, length us, event | category | flops | bytes accessed | tf_op | source)
XLA Modules:
  0.0 235.8 jit_solution(7843654203458309220)
XLA Ops:
  7.2 0.0 reduce-scatter.5.cloned.1.call-start
  7.2 11.9 %all_gather.3 = bf16[128,2048]{1,0:T(8,128)(2,1)S(1)} all-gather(bf16[32,2048]{1,0:T(8,128)(2,1)} %param.6), channel_id=1, replica_groups=mesh['dp'=8,'tensor'=4] {'tensor'}, dimensions={0}, use_global_device_ids=true | all-gather | bytes 655360 | tf_op jit(solution)/shard_map/all_gather | solution.py:10
  19.1 6.2 %fusion.5 = (bf16[128,2048]{1,0:T(8,128)(2,1)}, bf16[128,2048]{1,0:T(8,128)(2,1)S(1)}) fusion(bf16[128,2048]{1,0:T(8,128)(2,1)} %param.9, bf16[128,2048]{1,0:T(8,128)(2,1)} %param.8, bf16[128,2048]{1,0:T(8,128)(2,1)S(1)} %all_gather.3, bf16[2048,2048]{1,0:T(8,128)(2,1)} %param.7), kind=kOutput, calls=%fused_computation.12 | convolution fusion | flops 1077673984 | bytes 11010048 | tf_op jit(solution)/shard_map/dot_general | solution.py:11
  25.3 8.1 %convert_bitcast_fusion = f32[2048,2048]{0,1:T(8,128)} fusion(bf16[128,2048]{1,0:T(8,128)(2,1)S(1)} %get-tuple-element.14, bf16[128,2048]{1,0:T(8,128)(2,1)S(1)} %all_gather.3), kind=kOutput, calls=%fused_computation | convolution fusion | flops 1082130432 | bytes 17825792 | tf_op jit(solution)/shard_map/dot_general | solution.py:29
  33.4 0.0 reduce-scatter.5.cloned.1.call-update
  33.4 0.0 copy-start.1
  33.4 0.0 reduce-scatter.3.cloned.1.call-start
  33.5 7.1 %convolution_convert_fusion = bf16[128,2048]{1,0:T(8,128)(2,1)} fusion(bf16[128,2048]{1,0:T(8,128)(2,1)S(1)} %get-tuple-element.14, bf16[2048,2048]{1,0:T(8,128)(2,1)} %param.7), kind=kOutput, calls=%fused_computation.1 | convolution fusion | flops 1074003968 | bytes 9437184 | tf_op jit(solution)/shard_map/dot_general | solution.py:22
  40.6 0.0 reduce-scatter.3.cloned.1.call-update
  40.6 0.0 copy-done.1
  40.6 0.5 copy.11
  41.2 2.3 copy.12
  43.4 158.6 %reduce-scatter.5.cloned.1.call-done = f32[256,2048]{0,1:T(8,128)} async-done(((f32[2048,2048]{0,1:T(8,128)}), f32[256,2048]{0,1:T(8,128)}) %reduce-scatter.5.cloned.1.call-update) | async-done | bytes 2097168 | tf_op jit(solution)/shard_map/reduce_scatter | solution.py:32
  202.0 4.6 %add_divide_fusion = (f32[256,2048]{0,1:T(8,128)S(1)}, bf16[256,2048]{0,1:T(8,128)(2,1)}, bf16[256,2048]{0,1:T(8,128)(2,1)}) fusion(f32[256,2048]{0,1:T(8,128)} %reduce-scatter.5.cloned.1.call-done, bf16[256,2048]{0,1:T(8,128)(2,1)S(1)} %copy.11, bf16[256,2048]{0,1:T(8,128)(2,1)} %copy.12), kind=kLoop, calls=%fused_computation.2 | loop fusion | flops 7340032 | bytes 8388608 | tf_op jit(solution)/shard_map/div | solution.py:39
  206.6 0.0 copy-start
  206.6 2.4 copy.13
  208.9 0.0 copy-done
  208.9 1.4 copy.14
  210.4 1.8 copy.15
  212.2 16.8 %reduce-scatter.3.cloned.1.call-done = bf16[32,2048]{1,0:T(8,128)(2,1)} async-done(((bf16[128,2048]{1,0:T(8,128)(2,1)}), bf16[32,2048]{1,0:T(8,128)(2,1)}) %reduce-scatter.3.cloned.1.call-update) | async-done | bytes 131088 | tf_op jit(solution)/shard_map/reduce_scatter | solution.py:21
Async XLA Ops:
  7.2 194.8 %reduce-scatter.5.cloned.1.call-start = ((), (), s32[]{:S(2)}) async-start(), calls=%async_computation.3 | async-start | bytes 18874368 | tf_op jit(solution)/shard_map/reduce_scatter | solution.py:32
  33.4 7.2 %copy-start.1 = (bf16[256,2048]{1,0:T(8,128)(2,1)S(1)}, bf16[256,2048]{1,0:T(8,128)(2,1)}, u32[]{:S(2)}) copy-start(bf16[256,2048]{1,0:T(8,128)(2,1)} %param.10) | copy-start | bytes 3145732
  33.4 195.5 %reduce-scatter.3.cloned.1.call-start = ((), (), s32[]{:S(2)}) async-start(), calls=%async_computation.2 | async-start | bytes 655360 | tf_op jit(solution)/shard_map/reduce_scatter | solution.py:21
  206.6 2.4 copy-start
Sparse Core Ops, SparseCore 0:
  33.5 168.4 reduce-scatter.4
  205.4 23.5 reduce-scatter.2
where the time goes:
time: 236 us
  waiting for transfers between devices  175 us (74%)
  matrix products  21.4 us (9%)
  between operations  14.1 us (6%)
  blocking collectives  11.9 us (5%)
  local copies, waits for them, and re-layouts  8.37 us (4%)
  other arithmetic  4.59 us (2%)
    reduce_scatter x1, waiting for transfers between devices, local(): lax.psum_scatter(partial_value.astype(jnp.float32), 'dp', scatter_dimensi...  159 us
    reduce_scatter x1, waiting for transfers between devices, local(): lax.psum_scatter(lax.dot_general(gate_grad, gate_weight, (((1,), (1,)), (...  16.8 us
    all_gather x1, blocking collectives, local(): gathered = lax.all_gather(tokens, 'tensor', axis=0, tiled=True)  11.9 us
    unnamed x9, local copies, waits for them, and re-layouts  8.37 us
    dot_general x1, matrix products, local(): lax.dot_general(gathered, gate_grad, (((0,), (0,)), ((), ())), preferred_...  8.09 us
    dot_general x1, matrix products, local(): lax.dot_general(gate_grad, gate_weight, (((1,), (1,)), ((), ())), preferr...  7.13 us
    dot_general x1, matrix products, local(): jnp.dot(gathered, gate_weight, preferred_element_type=jnp.float32)  6.2 us
  transfers between devices with their start and end apart: 2, of which 2 were waited for; matrix products, arithmetic and copies ran while one was open for 9% of the time, Pallas kernels for 0%

commit v1 on v0

v1 whole, which is shorter than its diff:
```python
import functools
import math

import jax
import jax.numpy as jnp
from jax import lax
from jax.experimental import pallas as pl
from jax.experimental.pallas import tpu as pltpu
from jax.sharding import PartitionSpec as P

MESH = pl.DeviceIdType.MESH
F32, BF16 = jnp.float32, jnp.bfloat16
CORES = 2
WIDE = 256
VMEM_BUDGET = 60 * 2**20


def adam(grad, moment1, moment2):
    first = 0.9 * moment1.astype(F32) + 0.1 * grad
    second = 0.95 * moment2.astype(F32) + 0.05 * grad * grad
    return first, second, first / (jnp.sqrt(second) + 1e-08)


def activation_grads(gate_pre, cot, up):
    sig = jax.nn.sigmoid(gate_pre)
    cot = cot.astype(F32)
    up_grad = (cot * gate_pre * sig).astype(BF16)
    gate_grad = (cot * up.astype(F32) * sig * (1.0 + gate_pre * (1.0 - sig))).astype(BF16)
    return up_grad, gate_grad


def kernel(ndp, nt, tok, w, up, cot, m1, m2, in_grad, up_grad, nm1, nm2, upd,
           tg, xg, xt, wv, upv, cotv, m1v, m2v, gall, term, termr,
           loc_sem, w_sem, tg_s, tg_r, x1_s, x1_r, x2_s, x2_r,
           us, ur, ds, dr, ps, pr, qs, qr, ts, tr):
    d, t = lax.axis_index("dp"), lax.axis_index("tensor")
    z, core = d // CORES, d % CORES
    nz = ndp // CORES
    mate = d + 1 - 2 * core
    m, dw = tok.shape
    g, hid = up.shape
    rw = m1.shape[0]
    nc, _, hc = wv.shape
    scale = 1.0 / math.sqrt(ndp * g)

    def rdma(src, dst, s, r, dp, tn):
        return pltpu.make_async_remote_copy(
            src_ref=src, dst_ref=dst, send_sem=s, recv_sem=r, device_id=(dp, tn), device_id_type=MESH)

    mine = pl.ds(pl.multiple_of(t * m, m), m)
    loads = [
        pltpu.make_async_copy(tok, tg.at[mine], loc_sem.at[0]),
        pltpu.make_async_copy(tok.at[:, pl.ds(pl.multiple_of(d * rw, rw), rw)], xg.at[d, t], loc_sem.at[1]),
        pltpu.make_async_copy(cot, cotv, loc_sem.at[2]),
        pltpu.make_async_copy(up, upv, loc_sem.at[3]),
        pltpu.make_async_copy(m1, m1v, loc_sem.at[4]),
        pltpu.make_async_copy(m2, m2v, loc_sem.at[5]),
    ]

    def w_load(c):
        return pltpu.make_async_copy(w.at[:, pl.ds(pl.multiple_of(c * hc, hc), hc)], wv.at[c], w_sem.at[c])

    loads[0].start()
    loads[1].start()
    w_load(0).start()
    loads[2].start()
    loads[3].start()
    for c in range(1, nc):
        w_load(c).start()
    loads[4].start()
    loads[5].start()

    barrier = pltpu.get_barrier_semaphore()
    for k in range(1, nt):
        pl.semaphore_signal(barrier, inc=1, device_id=(d, lax.rem(t + k, nt)), device_id_type=MESH)
    for k in range(1, ndp):
        pl.semaphore_signal(barrier, inc=1, device_id=(lax.rem(d + k, ndp), t), device_id_type=MESH)
    loads[0].wait()
    loads[1].wait()
    pl.semaphore_wait(barrier, nt - 1 + ndp - 1)

    def tok_copy(k):
        return rdma(tg.at[mine], tg.at[mine], tg_s.at[k], tg_r.at[k], d, lax.rem(t + k, nt))

    def tok_recv(k):
        rows = pl.ds(pl.multiple_of(lax.rem(t + nt - k, nt) * m, m), m)
        return rdma(tg.at[rows], tg.at[rows], tg_s.at[k], tg_r.at[k], d, lax.rem(t + k, nt))

    def x1_copy(k):
        to = lax.rem(d + k, ndp)
        return rdma(tg.at[mine, pl.ds(pl.multiple_of(to * rw, rw), rw)], xg.at[d, t], x1_s.at[k], x1_r.at[k], to, t)

    def x1_recv(k):
        origin = lax.rem(d + ndp - k, ndp)
        return rdma(xg.at[origin, t], xg.at[origin, t], x1_s.at[k], x1_r.at[k], lax.rem(d + k, ndp), t)

    def x2_copy(k):
        return rdma(xg.at[:, t], xg.at[:, t], x2_s.at[k], x2_r.at[k], d, lax.rem(t + k, nt))

    def x2_recv(k):
        origin = lax.rem(t + nt - k, nt)
        return rdma(xg.at[:, origin], xg.at[:, origin], x2_s.at[k], x2_r.at[k], d, lax.rem(t + k, nt))

    for k in range(1, nt):
        tok_copy(k).start()
    for k in range(1, ndp):
        x1_copy(k).start()
    loads[2].wait()
    loads[3].wait()
    for k in range(1, nt):
        tok_recv(k).wait_recv()

    def block(c, chip, cr):
        return gall.at[c, pl.ds(pl.multiple_of((chip * CORES + cr) * g, g), g)]

    def up_copy(s, c):
        b = block(c, z - s, core)
        return rdma(b, b, us.at[s, c], ur.at[s, c], d + CORES, t)

    def down_copy(s, c):
        b = block(c, z + s, core)
        return rdma(b, b, ds.at[s, c], dr.at[s, c], d - CORES, t)

    def up_recv(s, c):
        b = block(c, z - s, core)
        return rdma(b, b, us.at[s - 1, c], ur.at[s - 1, c], d + CORES, t)

    def down_recv(s, c):
        b = block(c, z + s, core)
        return rdma(b, b, ds.at[s - 1, c], dr.at[s - 1, c], d - CORES, t)

    def mate_copy(s, c, low):
        b = block(c, z - s if low else z + s, core)
        return rdma(b, b, (ps if low else qs).at[s, c], (pr if low else qr).at[s, c], mate, t)

    def mate_recv(s, c, low):
        b = block(c, z - s if low else z + s, 1 - core)
        return rdma(b, b, (ps if low else qs).at[s, c], (pr if low else qr).at[s, c], mate, t)

    def hop(s, c):
        @pl.when(z - s >= 0)
        def _():
            if s > 0:
                up_recv(s, c).wait_recv()
            if s < nz - 1:
                @pl.when(z + 1 < nz)
                def _():
                    up_copy(s, c).start()
            mate_copy(s, c, True).start()

        @pl.when(z + s < nz)
        def _():
            if s > 0:
                down_recv(s, c).wait_recv()
            if s < nz - 1:
                @pl.when(z >= 1)
                def _():
                    down_copy(s, c).start()
            if s > 0:
                mate_copy(s, c, False).start()

    @pl.loop(0, nc)
    def _(c):
        w_load(c).wait()
        cols = pl.ds(pl.multiple_of(c * hc, hc), hc)
        gate_pre = jnp.dot(tg[...], wv[c], preferred_element_type=F32)
        ug, gg = activation_grads(gate_pre, cotv[:, cols], upv[:, cols])
        gall[c, pl.ds(pl.multiple_of(d * g, g), g), :] = gg
        up_grad[:, cols] = ug
        hop(0, c)

    for k in range(1, ndp):
        x1_recv(k).wait_recv()
    for k in range(1, nt):
        x2_copy(k).start()

    part = dw // nc

    @pl.loop(0, nc)
    def _(n):
        if nz > 1:
            hop(1, n)
        rows = pl.ds(pl.multiple_of(n * part, part), part)
        own = pl.ds(pl.multiple_of(d * g, g), g)
        total = jnp.zeros((g, part), F32)
        for c in range(nc):
            total += lax.dot_general(
                gall[c, own, :], wv[c, rows, :], (((1,), (1,)), ((), ())), preferred_element_type=F32)
        term[:, rows] = total.astype(BF16)

    for k in range(1, nt):
        x2_recv(k).wait_recv()
    for i in range(ndp):
        xt[:, i * g:(i + 1) * g] = xg[i].reshape(g, rw).T

    def term_copy(k):
        to = lax.rem(t + k, nt)
        return rdma(term.at[pl.ds(pl.multiple_of(to * m, m), m)], termr.at[k], ts.at[k], tr.at[k], d, to)

    for k in range(1, nt):
        term_copy(k).start()
    for s in range(2, nz - 1):
        @pl.loop(0, nc)
        def _(c):
            hop(s, c)
    total = term[mine, :].astype(F32)
    for k in range(1, nt):
        term_copy(k).wait_recv()
        total += termr[k].astype(F32)
    in_grad[...] = total.astype(BF16)
    loads[4].wait()
    loads[5].wait()

    @pl.loop(0, nc)
    def _(c):
        if nz > 2:
            hop(nz - 1, c)
        for s in range(nz):
            @pl.when(z - s >= 0)
            def _():
                mate_recv(s, c, True).wait_recv()
            if s > 0:
                @pl.when(z + s < nz)
                def _():
                    mate_recv(s, c, False).wait_recv()
        cols = pl.ds(pl.multiple_of(c * hc, hc), hc)
        grad = jnp.dot(xt[...], gall[c], preferred_element_type=F32) * scale
        first, second, step = adam(grad, m1v[:, cols], m2v[:, cols])
        nm1[:, cols] = first.astype(BF16)
        nm2[:, cols] = second.astype(BF16)
        upd[:, cols] = step

    for k in range(1, nt):
        tok_copy(k).wait_send()
        x2_copy(k).wait_send()
        term_copy(k).wait_send()
    for k in range(1, ndp):
        x1_copy(k).wait_send()

    @pl.loop(0, nc)
    def _(c):
        for s in range(nz):
            @pl.when(z - s >= 0)
            def _():
                mate_copy(s, c, True).wait_send()
                if s < nz - 1:
                    @pl.when(z + 1 < nz)
                    def _():
                        up_copy(s, c).wait_send()

            @pl.when(z + s < nz)
            def _():
                if s > 0:
                    mate_copy(s, c, False).wait_send()
                if s < nz - 1:
                    @pl.when(z >= 1)
                    def _():
                        down_copy(s, c).wait_send()


def fused(ndp, nt, tokens, gate_weight, up_act, cotangent, moment1, moment2):
    m, dw = tokens.shape
    g, hid = up_act.shape
    rw = moment1.shape[0]
    nc, nz = hid // WIDE, ndp // CORES
    any_spec, vmem = pl.BlockSpec(memory_space=pl.ANY), pl.BlockSpec(memory_space=pltpu.VMEM)
    dma = pltpu.SemaphoreType.DMA
    return pl.pallas_call(
        functools.partial(kernel, ndp, nt),
        out_shape=(
            jax.ShapeDtypeStruct((m, dw), BF16),
            jax.ShapeDtypeStruct((g, hid), BF16),
            jax.ShapeDtypeStruct((rw, hid), BF16),
            jax.ShapeDtypeStruct((rw, hid), BF16),
            jax.ShapeDtypeStruct((rw, hid), F32),
        ),
        in_specs=[any_spec] * 6,
        out_specs=(vmem,) * 5,
        scratch_shapes=[
            pltpu.VMEM((g, dw), BF16),
            pltpu.VMEM((ndp, nt, m, rw), BF16),
            pltpu.VMEM((rw, ndp * g), BF16),
            pltpu.VMEM((nc, dw, WIDE), BF16),
            pltpu.VMEM((g, hid), BF16),
            pltpu.VMEM((g, hid), BF16),
            pltpu.VMEM((rw, hid), BF16),
            pltpu.VMEM((rw, hid), BF16),
            pltpu.VMEM((nc, ndp * g, WIDE), BF16),
            pltpu.VMEM((g, dw), BF16),
            pltpu.VMEM((nt, m, dw), BF16),
            dma((6,)), dma((nc,)),
            dma((nt,)), dma((nt,)),
            dma((ndp,)), dma((ndp,)),
            dma((nt,)), dma((nt,)),
            dma((nz, nc)), dma((nz, nc)), dma((nz, nc)), dma((nz, nc)),
            dma((nz, nc)), dma((nz, nc)), dma((nz, nc)), dma((nz, nc)),
            dma((nt,)), dma((nt,)),
        ],
        compiler_params=pltpu.CompilerParams(
            collective_id=0, has_side_effects=True, vmem_limit_bytes=VMEM_BUDGET),
    )(tokens, gate_weight, up_act, cotangent, moment1, moment2)


def plain(ndp, nt, tokens, gate_weight, up_act, cotangent, moment1, moment2):
    gathered = lax.all_gather(tokens, "tensor", axis=0, tiled=True)
    gate_pre = jnp.dot(gathered, gate_weight, preferred_element_type=F32)
    up_grad, gate_grad = activation_grads(gate_pre, cotangent, up_act)
    term = lax.dot_general(
        gate_grad, gate_weight, (((1,), (1,)), ((), ())), preferred_element_type=F32).astype(BF16)
    in_grad = lax.psum_scatter(term, "tensor", scatter_dimension=0, tiled=True)
    partial_value = lax.dot_general(
        gathered, gate_grad, (((0,), (0,)), ((), ())), preferred_element_type=F32).astype(BF16)
    shard = lax.psum_scatter(partial_value.astype(F32), "dp", scatter_dimension=0, tiled=True)
    first, second, update = adam(shard * (1.0 / math.sqrt(ndp * gathered.shape[0])), moment1, moment2)
    return in_grad, up_grad, first.astype(BF16), second.astype(BF16), update


def local(ndp, nt, *args):
    (m, dw), (g, hid), rw = args[0].shape, args[2].shape, args[4].shape[0]
    need = (2 * dw * hid + 2 * ndp * g * (hid + 2 * rw) + 12 * g * hid + 16 * rw * hid + 16 * g * dw)
    fits = (need <= VMEM_BUDGET and ndp % CORES == 0 and ndp > CORES and nt > 1 and hid % WIDE == 0
            and g % 128 == 0 and rw % 128 == 0 and m % 16 == 0 and dw % (128 * (hid // WIDE)) == 0)
    return (fused if fits else plain)(ndp, nt, *args)


def solution(mesh):
    both = P("dp", "tensor")
    rows = P(("dp", "tensor"), None)
    return jax.shard_map(
        functools.partial(local, mesh.shape["dp"], mesh.shape["tensor"]),
        mesh=mesh,
        in_specs=(rows, P(None, "tensor"), both, both, both, both),
        out_specs=(rows, both, both, both, both),
        check_vma=False,
    )
```

time: 236 us -> 65.5 us (0.28)
  waiting for transfers between devices: 175 us -> 0 us
  Pallas kernels: 0 us -> 56.3 us
  matrix products: 21.4 us -> 0 us
  between operations: 14.1 us -> 0.65 us
  blocking collectives: 11.9 us -> 0 us
  other arithmetic: 4.59 us -> 0 us
    reduce_scatter x2 -> x0, waiting for transfers between devices: 175 us -> none  [the longest x1 159 us: local(): lax.psum_scatter(partial_value.astype(jnp.float32), 'dp', scatter_dimensi...]
    pallas_call x0 -> x1, Pallas kernels: none -> 56.3 us  [fused(): pl.pallas_call(functools.partial(kernel, ndp, nt), out_shape=(jax.ShapeDt...]
    dot_general x3 -> x0, matrix products: 21.4 us -> none  [the longest x1 8.09 us: local(): lax.dot_general(gathered, gate_grad, (((0,), (0,)), ((), ())), preferred_...]
    all_gather x1 -> x0, blocking collectives: 11.9 us -> none  [local(): gathered = lax.all_gather(tokens, 'tensor', axis=0, tiled=True)]
    div x1 -> x0, other arithmetic: 4.59 us -> none  [local(): update = first / (jnp.sqrt(second) + 1e-08)]
  transfers between devices with their start and end apart: 2 -> 0, of which waited for: 2 -> 0; matrix products, arithmetic and copies ran while one was open for 9% -> 0% of each run, Pallas kernels for 0% -> 0%
where the time goes in v1:
time: 65.5 us; the launch traced here: 65.3 us
  Pallas kernels  56.3 us (86%)
  local copies, waits for them, and re-layouts  8.29 us (13%)
    pallas_call x1, Pallas kernels, fused(): pl.pallas_call(functools.partial(kernel, ndp, nt), out_shape=(jax.ShapeDt...  56.3 us
    unnamed x9, local copies, waits for them, and re-layouts  8.29 us

profile of v1, /device:TPU:0, one launch (start us, length us, event | category | flops | bytes accessed | tf_op | source)
XLA Modules:
  0.0 65.3 jit_solution(4952888476318545232)
XLA Ops:
  0.6 56.3 %shard_map.101 = (bf16[32,2048]{1,0:T(8,128)(2,1)}, bf16[128,2048]{1,0:T(8,128)(2,1)}, bf16[256,2048]{1,0:T(8,128)(2,1)}, bf16[256,2048]{1,0:T(8,128)(2,1)}, f32[256,2048]{1,0:T(8,128)}) custom-call(bf16[32,2048]{1,0:T(8,128)(2,1)} %tok.1, bf16[2048,2048]{1,0:T(8,128)(2,1)} %w.1, bf16[128,2048]{1,0:T(8,128)(2,1)} %up.1, bf16[128,2048]{1,0:T(8,128)(2,1)} %cot.1, ...), custom_call_target="tpu_custom_call" | custom-call | tf_op jit(solution)/shard_map/pallas_call | solution.py:268
  57.0 0.0 copy-start.1
  57.0 1.7 %copy.16 = bf16[32,2048]{1,0:T(8,128)(2,1)} copy(bf16[32,2048]{1,0:T(8,128)(2,1)} %get-tuple-element.10) | data formatting | bytes 262144
  58.6 1.9 %copy.17 = bf16[128,2048]{1,0:T(8,128)(2,1)} copy(bf16[128,2048]{1,0:T(8,128)(2,1)} %get-tuple-element.11) | data formatting | bytes 1048576
  60.5 0.0 copy-start
  60.5 2.5 %copy.18 = bf16[256,2048]{1,0:T(8,128)(2,1)} copy(bf16[256,2048]{1,0:T(8,128)(2,1)} %get-tuple-element.12) | data formatting | bytes 2097152
  63.0 0.0 copy-done.1
  63.0 1.0 %copy.19 = bf16[256,2048]{1,0:T(8,128)(2,1)} copy(bf16[256,2048]{1,0:T(8,128)(2,1)S(1)} %copy-done.1) | data formatting | bytes 2097152
  64.0 0.0 copy-done
  64.0 1.3 %copy.20 = f32[256,2048]{1,0:T(8,128)} copy(f32[256,2048]{1,0:T(8,128)S(1)} %copy-done) | data formatting | bytes 4194304
Async XLA Ops:
  57.0 6.0 %copy-start.1 = (bf16[256,2048]{1,0:T(8,128)(2,1)S(1)}, bf16[256,2048]{1,0:T(8,128)(2,1)}, u32[]{:S(2)}) copy-start(bf16[256,2048]{1,0:T(8,128)(2,1)} %get-tuple-element.13) | copy-start | bytes 3145732
  60.5 3.4 %copy-start = (f32[256,2048]{1,0:T(8,128)S(1)}, f32[256,2048]{1,0:T(8,128)}, u32[]{:S(2)}) copy-start(f32[256,2048]{1,0:T(8,128)} %get-tuple-element.14) | copy-start | bytes 6291460

commit v2 on v1

--- a/solution.py
+++ b/solution.py
@@ -12,7 +12,7 @@
 F32, BF16 = jnp.float32, jnp.bfloat16
 CORES = 2
 WIDE = 256
-VMEM_BUDGET = 60 * 2**20
+VMEM_BUDGET = 48 * 2**20
 
 
 def adam(grad, moment1, moment2):
@@ -263,17 +263,12 @@
     g, hid = up_act.shape
     rw = moment1.shape[0]
     nc, nz = hid // WIDE, ndp // CORES
-    any_spec, vmem = pl.BlockSpec(memory_space=pl.ANY), pl.BlockSpec(memory_space=pltpu.VMEM)
+    any_spec, vmem = pl.BlockSpec(memory_space=pltpu.HBM), pl.BlockSpec(memory_space=pltpu.VMEM)
     dma = pltpu.SemaphoreType.DMA
-    return pl.pallas_call(
+    results = (((m, dw), BF16), ((g, hid), BF16), ((rw, hid), BF16), ((rw, hid), BF16), ((rw, hid), F32))
+    held = pl.pallas_call(
         functools.partial(kernel, ndp, nt),
-        out_shape=(
-            jax.ShapeDtypeStruct((m, dw), BF16),
-            jax.ShapeDtypeStruct((g, hid), BF16),
-            jax.ShapeDtypeStruct((rw, hid), BF16),
-            jax.ShapeDtypeStruct((rw, hid), BF16),
-            jax.ShapeDtypeStruct((rw, hid), F32),
-        ),
+        out_shape=tuple(pltpu.VMEM(shape, dtype) for shape, dtype in results),
         in_specs=[any_spec] * 6,
         out_specs=(vmem,) * 5,
         scratch_shapes=[
@@ -298,7 +293,25 @@
         ],
         compiler_params=pltpu.CompilerParams(
             collective_id=0, has_side_effects=True, vmem_limit_bytes=VMEM_BUDGET),
-    )(tokens, gate_weight, up_act, cotangent, moment1, moment2)
+    )(*(pltpu.with_memory_space_constraint(x, pltpu.HBM)
+        for x in (tokens, gate_weight, up_act, cotangent, moment1, moment2)))
+    return pl.pallas_call(
+        write_out,
+        out_shape=tuple(pltpu.HBM(shape, dtype) for shape, dtype in results),
+        in_specs=[vmem] * 5,
+        out_specs=(any_spec,) * 5,
+        scratch_shapes=[dma((5,))],
+        compiler_params=pltpu.CompilerParams(vmem_limit_bytes=2**20),
+    )(*(pltpu.with_memory_space_constraint(x, pltpu.VMEM) for x in held))
+
+
+def write_out(*refs):
+    sems = refs[-1]
+    copies = [pltpu.make_async_copy(refs[i], refs[5 + i], sems.at[i]) for i in range(5)]
+    for copy in reversed(copies):
+        copy.start()
+    for copy in copies:
+        copy.wait()
 
 
 def plain(ndp, nt, tokens, gate_weight, up_act, cotangent, moment1, moment2):

time: 65.5 us -> 57.2 us (0.87)
  local copies, waits for them, and re-layouts: 8.29 us -> 0 us
    unnamed x9 -> x0, local copies, waits for them, and re-layouts: 8.29 us -> none
    pallas_call x1 -> x2, Pallas kernels: 56.3 us -> 56.4 us  [the longest x1 54.2 us: fused(): pl.pallas_call(functools.partial(kernel, ndp, nt), out_shape=tuple((pltpu...]
where the time goes in v2:
time: 57.2 us; the launch traced here: 57.1 us
  Pallas kernels  56.4 us (99%)
  between operations  0.64 us (1%)
    pallas_call x1, Pallas kernels, fused(): pl.pallas_call(functools.partial(kernel, ndp, nt), out_shape=tuple((pltpu...  54.2 us
    pallas_call x1, Pallas kernels, fused(): pl.pallas_call(write_out, out_shape=tuple((pltpu.HBM(shape, dtype) for sh...  2.24 us

profile of v2, /device:TPU:0, one launch (start us, length us, event | category | flops | bytes accessed | tf_op | source)
XLA Modules:
  0.0 57.1 jit_solution(6264669798131937436)
XLA Ops:
  0.6 54.2 %shard_map.101 = (bf16[32,2048]{1,0:T(8,128)(2,1)S(1)}, bf16[128,2048]{1,0:T(8,128)(2,1)S(1)}, bf16[256,2048]{1,0:T(8,128)(2,1)S(1)}, bf16[256,2048]{1,0:T(8,128)(2,1)S(1)}, f32[256,2048]{1,0:T(8,128)S(1)}) custom-call(bf16[32,2048]{1,0:T(8,128)(2,1)} %tok.1, bf16[2048,2048]{1,0:T(8,128)(2,1)} %w.1, bf16[128,2048]{1,0:T(8,128)(2,1)} %up.1, ...), custom_call_target="tpu_custom_call" | custom-call | tf_op jit(solution)/shard_map/pallas_call | solution.py:269
  54.8 2.2 %shard_map.102 = (bf16[32,2048]{1,0:T(8,128)(2,1)}, bf16[128,2048]{1,0:T(8,128)(2,1)}, bf16[256,2048]{1,0:T(8,128)(2,1)}, bf16[256,2048]{1,0:T(8,128)(2,1)}, f32[256,2048]{1,0:T(8,128)}) custom-call(bf16[32,2048]{1,0:T(8,128)(2,1)S(1)} %get-tuple-element.10.refs_0_, bf16[128,2048]{1,0:T(8,128)(2,1)S(1)} %get-tuple-element.11.refs_1_, ...), custom_call_target="tpu_custom_call" | custom-call | tf_op jit(solution)/shard_map/pallas_call | solution.py:298

commit v3 on v2

--- a/solution.py
+++ b/solution.py
@@ -11,7 +11,7 @@
 MESH = pl.DeviceIdType.MESH
 F32, BF16 = jnp.float32, jnp.bfloat16
 CORES = 2
-WIDE = 256
+WIDE = 512
 VMEM_BUDGET = 48 * 2**20
 
 

time: 57.2 us -> 55.2 us (0.965)
  Pallas kernels: 56.4 us -> 54.4 us
    pallas_call x1, Pallas kernels: 54.2 us -> 52.2 us  [fused(): pl.pallas_call(functools.partial(kernel, ndp, nt), out_shape=tuple((pltpu...]
where the time goes in v3:
time: 55.2 us; the launch traced here: 55.1 us
  Pallas kernels  54.4 us (99%)
  between operations  0.64 us (1%)
    pallas_call x1, Pallas kernels, fused(): pl.pallas_call(functools.partial(kernel, ndp, nt), out_shape=tuple((pltpu...  52.2 us
    pallas_call x1, Pallas kernels, fused(): pl.pallas_call(write_out, out_shape=tuple((pltpu.HBM(shape, dtype) for sh...  2.24 us

profile of v3, /device:TPU:0, one launch (start us, length us, event | category | flops | bytes accessed | tf_op | source)
XLA Modules:
  0.0 55.1 jit_solution(16665282431480594121)
XLA Ops:
  0.6 52.2 %shard_map.101 = (bf16[32,2048]{1,0:T(8,128)(2,1)S(1)}, bf16[128,2048]{1,0:T(8,128)(2,1)S(1)}, bf16[256,2048]{1,0:T(8,128)(2,1)S(1)}, bf16[256,2048]{1,0:T(8,128)(2,1)S(1)}, f32[256,2048]{1,0:T(8,128)S(1)}) custom-call(bf16[32,2048]{1,0:T(8,128)(2,1)} %tok.1, bf16[2048,2048]{1,0:T(8,128)(2,1)} %w.1, bf16[128,2048]{1,0:T(8,128)(2,1)} %up.1, ...), custom_call_target="tpu_custom_call" | custom-call | tf_op jit(solution)/shard_map/pallas_call | solution.py:269
  52.8 2.2 %shard_map.102 = (bf16[32,2048]{1,0:T(8,128)(2,1)}, bf16[128,2048]{1,0:T(8,128)(2,1)}, bf16[256,2048]{1,0:T(8,128)(2,1)}, bf16[256,2048]{1,0:T(8,128)(2,1)}, f32[256,2048]{1,0:T(8,128)}) custom-call(bf16[32,2048]{1,0:T(8,128)(2,1)S(1)} %get-tuple-element.10.refs_0_, bf16[128,2048]{1,0:T(8,128)(2,1)S(1)} %get-tuple-element.11.refs_1_, ...), custom_call_target="tpu_custom_call" | custom-call | tf_op jit(solution)/shard_map/pallas_call | solution.py:298
